TPU v7x, 32 devices: a whole 2x2x4 slice. The times are simulated.
32 devices in a mesh: dp: 8 (over y, x, core), mp: 4 (over z).
Axes of the slice: x: 2, y: 2, z: 4, core: 2. Of those that a mesh axis runs over, the one named last changes fastest.
Arguments:
- hidden: bfloat16 [16384, 13824], P('dp', 'mp'), may hold values from -6 to 6
- out_grad: bfloat16 [16384, 5120], P('dp', 'mp'), may hold values from -6 to 6
- proj_in: bfloat16 [64, 13824], P(None, 'mp'), may hold values from -0.0546875 to 0.0546875
- proj_out: bfloat16 [64, 5120], P(None, 'mp'), may hold values from -0.078125 to 0.078125
- segment_ids: int32 [8, 2048], P('dp'), may hold values from 0 to 15, never falling along the last dimension, each value on 1 to 1024 neighbouring positions
Outputs:
- features: float32 [128, 4096], P('dp')
- gram: float32 [4096, 4096], P(('dp', 'mp'))
Inputs may be any that keep to these rules, and one draw needn't show every extreme that they name: `segment_ids`: within each row the numbers never fall; each of the 16 numbers names 1 to 1024 tokens of the row.
All inputs are finite; a program needn't handle non-finite values.
Results may differ from a plain program's by a relative error of at most 0.0003.
Values sent between devices are 32-bit elements; how exact they have to be, the bound alone decides.
No kernel may reach another device: no remote copies, remote signals or barrier semaphores. Data moves between devices by JAX's collectives and lax.ppermute only.
A program may use at most 64 MiB of HBM per device.

v0:
```python
import jax
import jax.numpy as jnp
from jax import lax
from jax.sharding import PartitionSpec as P

EX_DEV = 16


def outer_sums(onehot, projected, width):
    inputs = projected[:, :width]
    outputs = projected[:, width:]
    weighted = onehot[:, :, None] * outputs[None, :, :]
    grads = jnp.einsum("eti,tj->eij", weighted, inputs, precision=lax.Precision.HIGHEST)
    return grads.reshape(onehot.shape[0], width * width)


def body(hidden, out_grad, proj_in, proj_out, segment_ids):
    width = proj_in.shape[0]
    examples = EX_DEV
    inputs = lax.dot_general(
        hidden, proj_in, (((1,), (1,)), ((), ())), preferred_element_type=jnp.float32
    )
    outputs = lax.dot_general(
        out_grad, proj_out, (((1,), (1,)), ((), ())), preferred_element_type=jnp.float32
    )
    projected = jnp.concatenate([inputs, outputs], axis=1)
    example_ids = segment_ids[0]
    onehot = (example_ids[None, :] == jnp.arange(examples, dtype=jnp.int32)[:, None]).astype(
        jnp.float32
    )
    counts = jnp.sum(onehot, axis=1)
    summed = lax.psum(projected, "mp")
    grads = outer_sums(onehot, summed, width)
    features = grads / jnp.sqrt(counts)[:, None]
    proj_size = width * width
    data_count = lax.axis_size("dp")
    model_count = lax.axis_size("mp")
    row_count = proj_size // (data_count * model_count)
    total_examples = examples * data_count
    col_first = (lax.axis_index("dp") * model_count + lax.axis_index("mp")) * row_count
    shard_piece = lax.all_gather(features, "dp", axis=0, tiled=True)
    left = lax.dynamic_slice_in_dim(shard_piece, col_first, row_count, 1)
    gram_rows = lax.dot_general(
        left,
        shard_piece,
        (((0,), (0,)), ((), ())),
        precision=lax.Precision.HIGHEST,
        preferred_element_type=jnp.float32,
    )
    return (features, gram_rows / total_examples)


def solution(mesh):
    placed = (P("dp", "mp"), P("dp", "mp"), P(None, "mp"), P(None, "mp"), P("dp", None))
    return jax.shard_map(
        body,
        mesh=mesh,
        in_specs=placed,
        out_specs=(P("dp", None), P(("dp", "mp"), None)),
        check_vma=False,
    )
```

profile of v0, /device:TPU:0, one launch (start us, length us, event | category | flops | bytes accessed | tf_op | source)
XLA Modules:
  0.0 124.1 jit_solution(2751535235130744079)
XLA Ops:
  7.2 0.0 copy-start
  7.2 0.0 copy-start.2
  7.2 0.0 all-reduce.2.cloned.1.call-start
  7.2 0.9 copy-done
  8.2 0.0 copy-start.1
  8.2 9.5 %fusion.8 = f32[2048,64]{0,1:T(8,128)S(1)} fusion(bf16[2048,3456]{1,0:T(8,128)(2,1)} %param.5, bf16[64,3456]{1,0:T(8,128)(2,1)S(1)} %copy-done), kind=kOutput, calls=%fused_computation.13 | convolution fusion | flops 905969664 | bytes 15122432 | tf_op jit(solution)/shard_map/dot_general | solution.py:20
  17.7 0.0 copy-done.2
  17.7 0.0 copy-done.1
  17.7 0.0 copy-start.3
  17.8 1.7 %fusion.9 = f32[2048,64]{0,1:T(8,128)S(1)} fusion(bf16[2048,1280]{1,0:T(8,128)(2,1)S(1)} %copy-done.1, bf16[64,1280]{1,0:T(8,128)(2,1)S(1)} %copy-done.2), kind=kOutput, calls=%fused_computation.14 | convolution fusion | flops 335544320 | bytes 5931008 | tf_op jit(solution)/shard_map/dot_general | solution.py:23
  19.4 1.1 pad_maximum_fusion
  20.5 0.0 all-reduce.2.cloned.1.call-update
  20.5 0.2 all-gather.2.cloned.1.call-start
  20.8 0.0 copy-done.3
  20.8 0.1 fusion.6
  20.9 54.4 %all-reduce.2.cloned.1.call-done = f32[2048,128]{0,1:T(8,128)} async-done(((f32[2048,128]{0,1:T(8,128)}), f32[2048,128]{0,1:T(8,128)}) %all-reduce.2.cloned.1.call-update) | async-done | bytes 1048592 | tf_op jit(solution)/shard_map/psum | solution.py:32
  75.4 1.1 slice.8
  76.4 7.7 %fusion = f32[16,64,64]{2,1,0:T(8,128)S(1)} fusion(f32[2048,64]{0,1:T(8,128)S(1)} %slice.8, f32[16,2048]{1,0:T(8,128)S(1)} %fusion.4, f32[2048,128]{0,1:T(8,128)} %all-reduce.2.cloned.1.call-done), kind=kOutput, calls=%fused_computation | convolution fusion | flops 1612709888 | bytes 1441792 | tf_op jit(solution)/shard_map/eti,tj->eij/dot_general | solution.py:13
  84.1 0.2 reshape.32
  84.3 0.8 broadcast_divide_fusion
  85.1 0.0 all-gather.2.cloned.1.call-update
  85.1 27.2 %all-gather.2.cloned.1.call-done = f32[128,4096]{1,0:T(8,128)} async-done(((f32[16,4096]{1,0:T(8,128)}), f32[128,4096]{1,0:T(8,128)}) %all-gather.2.cloned.1.call-update) | async-done | bytes 2097168 | tf_op jit(solution)/shard_map/all_gather | solution.py:41
  112.3 4.9 %convolution_multiply_fusion = f32[128,4096]{1,0:T(8,128)} fusion(f32[128,4096]{1,0:T(8,128)} %all-gather.2.cloned.1.call-done, s32[]{:T(128)S(6)} %select_n.3), kind=kOutput, calls=%fused_computation.2 | convolution fusion | flops 805830656 | bytes 4259844 | tf_op jit(solution)/shard_map/dot_general | solution.py:43
  (2 shorter events, 0.0 us)
Async XLA Ops:
  7.2 1.0 copy-start
  7.2 10.5 %copy-start.2 = (bf16[64,1280]{1,0:T(8,128)(2,1)S(1)}, bf16[64,1280]{1,0:T(8,128)(2,1)}, u32[]{:S(2)}) copy-start(bf16[64,1280]{1,0:T(8,128)(2,1)} %param.8) | copy-start | bytes 491524
  7.2 68.2 %all-reduce.2.cloned.1.call-start = ((), (), s32[]{:S(2)}) async-start(), calls=%async_computation | async-start | bytes 2097152 | tf_op jit(solution)/shard_map/psum | solution.py:32
  8.2 9.5 %copy-start.1 = (bf16[2048,1280]{1,0:T(8,128)(2,1)S(1)}, bf16[2048,1280]{1,0:T(8,128)(2,1)}, u32[]{:S(2)}) copy-start(bf16[2048,1280]{1,0:T(8,128)(2,1)} %param.6) | copy-start | bytes 15728644
  17.7 3.0 %copy-start.3 = (s32[1,2048]{1,0:T(1,128)S(1)}, s32[1,2048]{1,0:T(1,128)}, u32[]{:S(2)}) copy-start(s32[1,2048]{1,0:T(1,128)} %param.9) | copy-start | bytes 24580
  20.5 91.8 %all-gather.2.cloned.1.call-start = ((), (), s32[]{:S(2)}) async-start(), calls=%async_computation.1 | async-start | bytes 2359296 | tf_op jit(solution)/shard_map/all_gather | solution.py:41
Sparse Core Ops, SparseCore 0:
  20.6 54.6 all-reduce.1
  85.2 27.0 all-gather.1
where the time goes:
time: 124 us
  waiting for transfers between devices  81.7 us (66%)
  matrix products  23.8 us (19%)
  between operations  14.1 us (11%)
  local copies, waits for them, and re-layouts  2.24 us (2%)
  other arithmetic  2 us (2%)
    psum x1, waiting for transfers between devices, body(): summed = lax.psum(projected, 'mp')  54.4 us
    all_gather x1, waiting for transfers between devices, body(): shard_piece = lax.all_gather(features, 'dp', axis=0, tiled=True)  27.2 us
    dot_general x1, matrix products, body(): lax.dot_general(hidden, proj_in, (((1,), (1,)), ((), ())), preferred_elem...  9.53 us
    dot_general x1, matrix products, outer_sums(): jnp.einsum('eti,tj->eij', weighted, inputs, precision=lax.Precision.HIGHEST)  7.67 us
    dot_general x1, matrix products, body(): lax.dot_general(left, shard_piece, (((0,), (0,)), ((), ())), precision=la...  4.89 us
  transfers between devices with their start and end apart: 2, of which 2 were waited for; matrix products, arithmetic and copies ran while one was open for 0% of the time, Pallas kernels for 0%

commit v1 on v0

--- a/solution.py
+++ b/solution.py
@@ -29,7 +29,9 @@
         jnp.float32
     )
     counts = jnp.sum(onehot, axis=1)
-    summed = lax.psum(projected, "mp")
+    summed = projected
+    for hop in (1, 2):
+        summed = summed + lax.ppermute(summed, "mp", [(dev, dev ^ hop) for dev in range(4)])
     grads = outer_sums(onehot, summed, width)
     features = grads / jnp.sqrt(counts)[:, None]
     proj_size = width * width

time: 124 us -> 142 us (1.15)
  waiting for transfers between devices: 81.7 us -> 96.9 us
  starting transfers between devices: 0.26 us -> 5.99 us
    ppermute x0 -> x2, waiting for transfers between devices: none -> 67.9 us  [body(): lax.ppermute(summed, 'mp', [(dev, dev ^ hop) for dev in range(4)])]
    psum x1 -> x0, waiting for transfers between devices: 54.4 us -> none  [body(): summed = lax.psum(projected, 'mp')]
    ppermute x0 -> x2, starting transfers between devices: none -> 5.95 us  [body(): lax.ppermute(summed, 'mp', [(dev, dev ^ hop) for dev in range(4)])]
    all_gather x1, waiting for transfers between devices: 27.2 us -> 29 us  [body(): shard_piece = lax.all_gather(features, 'dp', axis=0, tiled=True)]
  transfers between devices with their start and end apart: 2 -> 3, of which waited for: 2 -> 3; matrix products, arithmetic and copies ran while one was open for 0% -> 0% of each run, Pallas kernels for 0% -> 0%
where the time goes in v1:
time: 142 us
  waiting for transfers between devices  96.9 us (68%)
  matrix products  22.7 us (16%)
  between operations  14.1 us (10%)
  starting transfers between devices  5.99 us (4%)
    ppermute x2, waiting for transfers between devices, body(): lax.ppermute(summed, 'mp', [(dev, dev ^ hop) for dev in range(4)])  67.9 us
    all_gather x1, waiting for transfers between devices, body(): shard_piece = lax.all_gather(features, 'dp', axis=0, tiled=True)  29 us
    dot_general x1, matrix products, body(): lax.dot_general(hidden, proj_in, (((1,), (1,)), ((), ())), preferred_elem...  9.52 us
    dot_general x1, matrix products, outer_sums(): jnp.einsum('eti,tj->eij', weighted, inputs, precision=lax.Precision.HIGHEST)  6.63 us
    ppermute x2, starting transfers between devices, body(): lax.ppermute(summed, 'mp', [(dev, dev ^ hop) for dev in range(4)])  5.95 us
    dot_general x1, matrix products, body(): lax.dot_general(left, shard_piece, (((0,), (0,)), ((), ())), precision=la...  4.9 us
  transfers between devices with their start and end apart: 3, of which 3 were waited for; matrix products, arithmetic and copies ran while one was open for 0% of the time, Pallas kernels for 0%

profile of v1, /device:TPU:0, one launch (start us, length us, event | category | flops | bytes accessed | tf_op | source)
XLA Modules:
  0.0 142.2 jit_solution(7573900422999648538)
XLA Ops:
  7.2 0.0 copy-start
  7.2 0.0 copy-start.2
  7.2 0.0 all-gather.2.cloned.1.call-start
  7.2 0.9 copy-done
  8.2 0.0 copy-start.1
  8.2 9.5 %fusion.9 = f32[2048,64]{0,1:T(8,128)S(1)} fusion(bf16[2048,3456]{1,0:T(8,128)(2,1)} %param.5, bf16[64,3456]{1,0:T(8,128)(2,1)S(1)} %copy-done), kind=kOutput, calls=%fused_computation.14 | convolution fusion | flops 905969664 | bytes 15122432 | tf_op jit(solution)/shard_map/dot_general | solution.py:20
  17.7 0.0 copy-done.2
  17.7 0.0 copy-done.1
  17.7 0.0 copy-start.3
  17.7 1.7 %fusion.10 = f32[2048,64]{0,1:T(8,128)S(1)} fusion(bf16[2048,1280]{1,0:T(8,128)(2,1)S(1)} %copy-done.1, bf16[64,1280]{1,0:T(8,128)(2,1)S(1)} %copy-done.2), kind=kOutput, calls=%fused_computation.15 | convolution fusion | flops 335544320 | bytes 5931008 | tf_op jit(solution)/shard_map/dot_general | solution.py:23
  19.4 0.1 pad_maximum_fusion
  19.5 3.1 %collective-permute-start = (f32[2048,128]{0,1:T(8,128)S(1)}, f32[2048,128]{0,1:T(8,128)S(1)}, u32[]{:S(2)}, u32[]{:S(2)}) collective-permute-start(f32[2048,128]{0,1:T(8,128)S(1)} %pad_maximum_fusion), channel_id=1, source_target_pairs={{0,1},{1,0},{2,3},{3,2},{4,5},{5,4},{6,7},{7,6},{8,9},{9,8},{10,11... | collective-permute-start | bytes 3145736 | tf_op jit(solution)/shard_map/ppermute | solution.py:34
  22.6 23.1 %collective-permute-done = f32[2048,128]{0,1:T(8,128)S(1)} collective-permute-done((f32[2048,128]{0,1:T(8,128)S(1)}, f32[2048,128]{0,1:T(8,128)S(1)}, u32[]{:S(2)}, u32[]{:S(2)}) %collective-permute-start) | collective-permute-done | bytes 1048608 | tf_op jit(solution)/shard_map/ppermute | solution.py:34
  45.8 0.1 fusion.8
  45.9 2.8 %collective-permute-start.1 = (f32[2048,128]{0,1:T(8,128)S(1)}, f32[2048,128]{0,1:T(8,128)S(1)}, u32[]{:S(2)}, u32[]{:S(2)}) collective-permute-start(f32[2048,128]{0,1:T(8,128)S(1)} %fusion.8), channel_id=1, source_target_pairs={{0,2},{1,3},{2,0},{3,1},{4,6},{5,7},{6,4},{7,5},{8,10},{9,11},{10,... | collective-permute-start | bytes 3145736 | tf_op jit(solution)/shard_map/ppermute | solution.py:34
  48.7 0.0 copy-done.3
  48.8 0.1 fusion.6
  48.9 44.8 %collective-permute-done.1 = f32[2048,128]{0,1:T(8,128)S(1)} collective-permute-done((f32[2048,128]{0,1:T(8,128)S(1)}, f32[2048,128]{0,1:T(8,128)S(1)}, u32[]{:S(2)}, u32[]{:S(2)}) %collective-permute-start.1) | collective-permute-done | bytes 1048608 | tf_op jit(solution)/shard_map/ppermute | solution.py:34
  93.7 0.2 add.13
  93.9 6.6 %fusion = f32[16,64,64]{2,1,0:T(8,128)S(1)} fusion(f32[2048,64]{0,1:T(8,128)S(1)} %slice.8, f32[16,2048]{1,0:T(8,128)S(1)} %fusion.4, f32[2048,128]{0,1:T(8,128)S(1)} %add.13), kind=kOutput, calls=%fused_computation | convolution fusion | flops 1612709888 | bytes 1441792 | tf_op jit(solution)/shard_map/eti,tj->eij/dot_general | solution.py:13
  100.5 0.2 reshape.32
  100.7 0.8 broadcast_divide_fusion
  101.5 0.0 all-gather.2.cloned.1.call-update
  101.5 29.0 %all-gather.2.cloned.1.call-done = f32[128,4096]{1,0:T(8,128)} async-done(((f32[16,4096]{1,0:T(8,128)}), f32[128,4096]{1,0:T(8,128)}) %all-gather.2.cloned.1.call-update) | async-done | bytes 2097168 | tf_op jit(solution)/shard_map/all_gather | solution.py:43
  130.5 4.9 %convolution_multiply_fusion = f32[128,4096]{1,0:T(8,128)} fusion(f32[128,4096]{1,0:T(8,128)} %all-gather.2.cloned.1.call-done, s32[]{:T(128)S(6)} %select_n.3), kind=kOutput, calls=%fused_computation.2 | convolution fusion | flops 805830656 | bytes 4259844 | tf_op jit(solution)/shard_map/dot_general | solution.py:45
  (3 shorter events, 0.1 us)
Async XLA Ops:
  7.2 1.0 copy-start
  7.2 10.5 %copy-start.2 = (bf16[64,1280]{1,0:T(8,128)(2,1)S(1)}, bf16[64,1280]{1,0:T(8,128)(2,1)}, u32[]{:S(2)}) copy-start(bf16[64,1280]{1,0:T(8,128)(2,1)} %param.8) | copy-start | bytes 491524
  7.2 123.3 %all-gather.2.cloned.1.call-start = ((), (), s32[]{:S(2)}) async-start(), calls=%async_computation | async-start | bytes 2359296 | tf_op jit(solution)/shard_map/all_gather | solution.py:43
  8.2 9.5 %copy-start.1 = (bf16[2048,1280]{1,0:T(8,128)(2,1)S(1)}, bf16[2048,1280]{1,0:T(8,128)(2,1)}, u32[]{:S(2)}) copy-start(bf16[2048,1280]{1,0:T(8,128)(2,1)} %param.6) | copy-start | bytes 15728644
  17.7 31.0 %copy-start.3 = (s32[1,2048]{1,0:T(1,128)S(1)}, s32[1,2048]{1,0:T(1,128)}, u32[]{:S(2)}) copy-start(s32[1,2048]{1,0:T(1,128)} %param.9) | copy-start | bytes 24580
  19.5 26.3 %collective-permute-start = (f32[2048,128]{0,1:T(8,128)S(1)}, f32[2048,128]{0,1:T(8,128)S(1)}, u32[]{:S(2)}, u32[]{:S(2)}) collective-permute-start(f32[2048,128]{0,1:T(8,128)S(1)} %pad_maximum_fusion), channel_id=1, source_target_pairs={{0,1},{1,0},{2,3},{3,2},{4,5},{5,4},{6,7},{7,6},{8,9},{9,8},{10,11... | collective-permute-start | bytes 3145736 | tf_op jit(solution)/shard_map/ppermute | solution.py:34
  45.9 47.7 %collective-permute-start.1 = (f32[2048,128]{0,1:T(8,128)S(1)}, f32[2048,128]{0,1:T(8,128)S(1)}, u32[]{:S(2)}, u32[]{:S(2)}) collective-permute-start(f32[2048,128]{0,1:T(8,128)S(1)} %fusion.8), channel_id=1, source_target_pairs={{0,2},{1,3},{2,0},{3,1},{4,6},{5,7},{6,4},{7,5},{8,10},{9,11},{10,... | collective-permute-start | bytes 3145736 | tf_op jit(solution)/shard_map/ppermute | solution.py:34
Sparse Core Ops, SparseCore 0:
  101.6 28.8 all-gather.1
